TPU v7x, 256 devices: a whole 4x4x8 slice. The times are simulated.
256 devices in a mesh: expert: 64 (over x, z, core), tensor: 4 (over y).
Axes of the slice: x: 4, y: 4, z: 8, core: 2. Of those that a mesh axis runs over, the one named last changes fastest.
Arguments:
- tokens: bfloat16 [8192, 3584], P('expert', 'tensor'), may hold values from -6 to 6
- expert_ids: int32 [8192, 4], P('expert'), may hold values from 0 to 63, all different within a row; in each aligned block of 128 rows (0 to 127, 128 to 255, ...) at most 12 rows name the same one
- gate_values: bfloat16 [8192, 4], P('expert'), may hold values from 0.049804688 to 0.3984375
- w_gate: bfloat16 [64, 3584, 1024], P('expert', None, 'tensor'), may hold values from -0.09375 to 0.09375
- w_up: bfloat16 [64, 3584, 1024], P('expert', None, 'tensor'), may hold values from -0.09375 to 0.09375
- w_down: bfloat16 [64, 1024, 3584], P('expert', 'tensor'), may hold values from -0.1875 to 0.1875
- shared_gate: bfloat16 [3584, 1024], P(None, 'tensor'), may hold values from -0.09375 to 0.09375
- shared_up: bfloat16 [3584, 1024], P(None, 'tensor'), may hold values from -0.09375 to 0.09375
- shared_down: bfloat16 [1024, 3584], P('tensor'), may hold values from -0.1875 to 0.1875
Outputs:
- moe_output: bfloat16 [8192, 3584], P('expert', 'tensor')
Inputs may be any that keep to these rules, and one draw needn't show every extreme that they name: `expert_ids`: each token names 4 different experts. Among the 128 tokens of one index of the expert axis (aligned blocks of 128 rows) no expert is named by more than 12 tokens, a bound that some block reaches.
All inputs are finite; a program needn't handle non-finite values.
Results may differ from a plain program's by a relative error of at most 0.013.
Values may be sent and summed in bfloat16 or wider, within the bound.
No kernel may reach another device: no remote copies, remote signals or barrier semaphores. Data moves between devices by JAX's collectives and lax.ppermute only.
A program may use at most 64 MiB of HBM per device.

v0:
```python
import jax
import jax.numpy as jnp
from jax import lax
from jax.sharding import Mesh
from jax.sharding import PartitionSpec as P

EXPERT = ("expert_0", "expert_1", "expert_2")


def in_order(tiles, dim):
    shape = list(tiles.shape[1:])
    shape[dim] *= tiles.shape[0]
    return jnp.moveaxis(tiles, 0, dim).reshape(shape)


def from_everyone(x, axis):
    copies = jnp.broadcast_to(x, (lax.axis_size(axis), *x.shape))
    return lax.all_to_all(copies, axis, split_axis=0, concat_axis=0, tiled=True)


def collect(x, axis, dim):
    return in_order(from_everyone(x, axis), dim)


def in_blocks(x, dim, devices):
    before, after = (x.shape[:dim], x.shape[dim + 1 :])
    return jnp.moveaxis(x.reshape(*before, devices, -1, *after), dim, 0)


def sent_and_summed(x, axis, dim):
    tiles = in_blocks(x, dim, lax.axis_size(axis))
    arrived = lax.all_to_all(tiles, axis, split_axis=0, concat_axis=0, tiled=True)
    return arrived.astype(jnp.float32).sum(axis=0)


def turned_blocks(tiles, axes, sequence):
    shape = [lax.axis_size(a) for a in axes]
    tiles = tiles.reshape(*shape, *tiles.shape[1:])
    for k in sequence:
        tiles = lax.all_to_all(tiles, axes[k], split_axis=k, concat_axis=k, tiled=True)
    return tiles.reshape(-1, *tiles.shape[len(axes) :])


def core_and_chips(x, groups, sequence, split_dim, concat_dim):
    devices = lax.axis_size(groups[0]) * lax.axis_size(groups[1])
    tiles = in_blocks(x, split_dim, devices)
    return in_order(turned_blocks(tiles, groups, sequence), concat_dim)


def per_device(
    tokens, expert_ids, gate_values, w_gate, w_up, w_down, shared_gate, shared_up, shared_down
):
    tok_dev, narrow = tokens.shape
    top_count = expert_ids.shape[1]
    per_lane, features, quarter = w_gate.shape
    lane_count = lax.axis_size(EXPERT)
    experts_all = lane_count * per_lane
    capacity = min(tok_dev, 3 * tok_dev * top_count // (2 * experts_all))
    total_rows = experts_all * capacity
    numbers = jnp.arange(experts_all, dtype=jnp.int32)
    onehot = (expert_ids[:, :, None] == numbers).astype(jnp.int32)
    per_token = jnp.sum(onehot, axis=1)
    earlier = jnp.cumsum(per_token, axis=0) - per_token
    slot_index = jnp.sum(onehot * earlier[:, None, :], axis=2)
    target = expert_ids * capacity + slot_index
    token_index = jnp.repeat(jnp.arange(tok_dev, dtype=jnp.int32), top_count)
    owners = jnp.full((total_rows,), tok_dev, jnp.int32).at[target.reshape(-1)].set(token_index)
    features_all = collect(tokens, "tensor", 1)
    shared_gate_sums = jnp.dot(features_all, shared_gate, preferred_element_type=jnp.float32)
    shared_up_sums = jnp.dot(features_all, shared_up, preferred_element_type=jnp.float32)
    shared_hidden = (jax.nn.silu(shared_gate_sums) * shared_up_sums).astype(jnp.bfloat16)
    shared_partial = jnp.dot(shared_hidden, shared_down, preferred_element_type=jnp.float32)
    padded = jnp.concatenate([tokens, jnp.zeros((1, narrow), jnp.bfloat16)], axis=0)
    outgoing = padded[owners].reshape(lane_count, per_lane * capacity, narrow)
    arrived = lax.all_to_all(outgoing, EXPERT, split_axis=0, concat_axis=0, tiled=True)
    arrived = arrived.reshape(lane_count, per_lane, capacity, narrow)
    block_rows = lax.all_gather(arrived, "tensor", axis=3, tiled=True)
    gate_more = jnp.einsum("sjcd,jdf->sjcf", block_rows, w_gate, preferred_element_type=jnp.float32)
    up_more = jnp.einsum("sjcd,jdf->sjcf", block_rows, w_up, preferred_element_type=jnp.float32)
    hidden = (jax.nn.silu(gate_more) * up_more).astype(jnp.bfloat16)
    partial_value = jnp.einsum("sjcf,jfd->sjcd", hidden, w_down, preferred_element_type=jnp.float32)
    summed = sent_and_summed(partial_value.astype(jnp.bfloat16), "tensor", 3)
    returned = core_and_chips(
        summed.reshape(lane_count, per_lane * capacity, narrow).astype(jnp.bfloat16),
        (("expert_0", "expert_1"), "expert_2"),
        (1, 0),
        0,
        0,
    ).astype(jnp.float32)
    picked = returned.reshape(total_rows, narrow)[target]
    routed = jnp.sum(gate_values.astype(jnp.float32)[:, :, None] * picked, axis=1)
    shared_total = sent_and_summed(shared_partial.astype(jnp.bfloat16), "tensor", 1)
    return (routed + shared_total).astype(jnp.bfloat16)


def solution(mesh):
    torus = Mesh(
        mesh.devices.reshape(4, 8, 2, mesh.shape["tensor"]),
        ("expert_0", "expert_1", "expert_2", "tensor"),
    )
    placed = (
        P(EXPERT, "tensor"),
        P(EXPERT, None),
        P(EXPERT, None),
        P(EXPERT, None, "tensor"),
        P(EXPERT, None, "tensor"),
        P(EXPERT, "tensor", None),
        P(None, "tensor"),
        P(None, "tensor"),
        P("tensor", None),
    )
    return jax.shard_map(
        per_device, mesh=torus, in_specs=placed, out_specs=P(EXPERT, "tensor"), check_vma=False
    )
```

profile of v0, /device:TPU:32, one launch (start us, length us, event | category | flops | bytes accessed | tf_op | source)
XLA Modules:
  0.0 321.1 jit_solution(12613605834629810689)
XLA Ops:
  6.5 0.8 convert_reduce_fusion.1
  7.7 0.7 select_reduce_fusion
  8.5 0.7 compare_select_fusion.2
  9.5 2.4 scatter_custom_fusion
  12.0 1.0 concatenate.3
  12.9 2.8 gather_fusion
  15.8 1.4 reshape.100
  17.2 56.0 %all_to_all.30 = bf16[64,12,896]{2,1,0:T(8,128)(2,1)S(1)} all-to-all(bf16[64,12,896]{2,1,0:T(8,128)(2,1)} %reshape.100), channel_id=1, replica_groups=mesh['expert_0'=4,'expert_1'=8,'expert_2'=2,'tensor'=4] {'expert_0','exp..., dimensions={0} | all-to-all | bytes 2752512 | tf_op jit(solution)/shard_map/all_to_all | solution.py:75
  73.2 1.4 copy.49
  74.9 1.1 broadcast_in_dim.25
  75.9 4.5 %all-to-all-start.4 = ((bf16[4,128,896]{1,2,0:T(8,128)(2,1)}), bf16[4,128,896]{1,2,0:T(8,128)(2,1)S(1)}, u32[]{:S(2)}, u32[]{:S(2)}) async-start(bf16[4,128,896]{1,2,0:T(8,128)(2,1)} %broadcast_in_dim.25), calls=%async_computation.4 | async-start | bytes 1835008 | tf_op jit(solution)/shard_map/all_to_all | solution.py:18
  80.4 58.3 %all-gather.3.cloned.1.call-done = bf16[64,12,3584]{2,0,1:T(8,128)(2,1)} async-done(((bf16[64,12,896]{2,0,1:T(8,128)(2,1)}), bf16[64,12,3584]{2,0,1:T(8,128)(2,1)}) %all-gather.3.cloned.1.call-update) | async-done | bytes 5505040 | tf_op jit(solution)/shard_map/all_gather | solution.py:77
  138.6 5.6 %fusion.5 = f32[64,1,12,256]{3,0,2,1:T(8,128)} fusion(bf16[64,12,3584]{2,0,1:T(8,128)(2,1)} %all-gather.3.cloned.1.call-done, bf16[1,3584,256]{2,1,0:T(8,128)(2,1)} %param.12), kind=kOutput, calls=%fused_computation.14 | convolution fusion | flops 1409286144 | bytes 8126464 | tf_op jit(solution)/shard_map/sjcd,jdf->sjcf/dot_general | solution.py:78
  144.3 11.5 %convolution_convert_fusion = bf16[64,12,3584]{2,0,1:T(8,128)(2,1)} fusion(bf16[1,256,3584]{2,1,0:T(8,128)(2,1)S(1)} %copy-done, bf16[64,12,3584]{2,0,1:T(8,128)(2,1)} %all-gather.3.cloned.1.call-done, bf16[1,3584,256]{2,1,0:T(8,128)(2,1)} %param.13, f32[64,1,12,256]{3,0,2,1:T(8,128)} %fusion.5), kind=kOutput, calls=%fused_computation.3 | convolution fusion | flops 2822504448 | bytes 15466496 | tf_op jit(solution)/shard_map/sjcf,jfd->sjcd/dot_general | solution.py:81
  155.7 5.8 %copy.65 = bf16[1,12,8,4,8,896]{5,4,2,1,0,3:T(8,128)(2,1)} copy(bf16[1,12,8,4,8,896]{5,4,3,2,1,0:T(8,128)(2,1)} %bitcast.85) | data formatting | bytes 11010048 | tf_op jit(solution)/shard_map/reshape | solution.py:27
  161.6 5.4 %all-to-all-start.1 = ((bf16[4,64,1,12,896]{4,1,3,2,0:T(8,128)(2,1)}), bf16[4,64,1,12,896]{4,1,3,2,0:T(8,128)(2,1)}, u32[]{:S(2)}, u32[]{:S(2)}) async-start(bf16[4,64,1,12,896]{4,1,3,2,0:T(8,128)(2,1)} %bitcast.82), calls=%async_computation.1 | async-start | bytes 11010048 | tf_op jit(solution)/shard_map/all_to_all | solution.py:32
  167.5 3.3 %convolution_convert_fusion.1 = bf16[128,3584]{1,0:T(8,128)(2,1)S(1)} fusion(bf16[256,3584]{1,0:T(8,128)(2,1)} %param.17, bf16[128,3584]{0,1:T(8,128)(2,1)S(1)} %bitcast.84, bf16[3584,256]{1,0:T(8,128)(2,1)} %param.16, f32[128,256]{1,0:T(8,128)S(1)} %fusion.39), kind=kOutput, calls=%fused_computation.5 | convolution fusion | flops 470417408 | bytes 5636096 | tf_op jit(solution)/shard_map/dot_general | solution.py:72
  170.8 1.0 copy.66
  171.8 58.3 %all-to-all-done.1 = bf16[4,64,1,12,896]{4,1,3,2,0:T(8,128)(2,1)} async-done(((bf16[4,64,1,12,896]{4,1,3,2,0:T(8,128)(2,1)}), bf16[4,64,1,12,896]{4,1,3,2,0:T(8,128)(2,1)}, u32[]{:S(2)}, u32[]{:S(2)}) %all-to-all-start.1) | async-done | bytes 5505056 | tf_op jit(solution)/shard_map/all_to_all | solution.py:32
  230.1 3.6 %reduce_sum.50 = bf16[64,12,896]{2,0,1:T(8,128)(2,1)S(1)} reduce(bf16[4,64,1,12,896]{4,1,3,2,0:T(8,128)(2,1)} %all-to-all-done.1, bf16[]{:T(256)} %constant.8.clone.1), dimensions={0,2}, to_apply=%region_4.5 | reduce | flops 2064384 | bytes 6881282 | tf_op jit(solution)/shard_map/reduce_sum | solution.py:33
  234.5 4.8 %all_to_all.31 = bf16[32,2,1,12,896]{4,0,3,2,1:T(8,128)(2,1)S(1)} all-to-all(bf16[32,2,1,12,896]{4,0,3,2,1:T(8,128)(2,1)S(1)} %copy.52), channel_id=1, replica_groups=mesh['expert_0'=4,'expert_1'=8,'expert_2'=2,'tensor'=4] {'expert_2'}, dimensions={1} | all-to-all | bytes 2752512 | tf_op jit(solution)/shard_map/all_to_all | solution.py:40
  239.3 3.5 %all-to-all-start.5 = ((bf16[4,128,896]{2,1,0:T(8,128)(2,1)}), bf16[4,128,896]{2,1,0:T(8,128)(2,1)S(1)}, u32[]{:S(2)}, u32[]{:S(2)}) async-start(bf16[4,128,896]{2,1,0:T(8,128)(2,1)} %bitcast.81), calls=%async_computation.5 | async-start | bytes 1835008 | tf_op jit(solution)/shard_map/all_to_all | solution.py:32
  242.8 2.5 copy.53
  245.3 11.7 %all-to-all-done.5 = bf16[4,128,896]{2,1,0:T(8,128)(2,1)S(1)} async-done(((bf16[4,128,896]{2,1,0:T(8,128)(2,1)}), bf16[4,128,896]{2,1,0:T(8,128)(2,1)S(1)}, u32[]{:S(2)}, u32[]{:S(2)}) %all-to-all-start.5) | async-done | bytes 917536 | tf_op jit(solution)/shard_map/all_to_all | solution.py:32
  257.1 6.9 %all-to-all-start.3 = ((bf16[32,2,1,12,896]{4,1,3,2,0:T(2,128)(2,1)}), bf16[32,2,1,12,896]{4,1,3,2,0:T(2,128)(2,1)S(1)}, u32[]{:S(2)}, u32[]{:S(2)}) async-start(bf16[32,2,1,12,896]{4,1,3,2,0:T(2,128)(2,1)} %copy.53), calls=%async_computation.3 | async-start | bytes 2752512 | tf_op jit(solution)/shard_map/all_to_all | solution.py:40
  264.4 34.2 %all-to-all-done.3 = bf16[32,2,1,12,896]{4,1,3,2,0:T(2,128)(2,1)S(1)} async-done(((bf16[32,2,1,12,896]{4,1,3,2,0:T(2,128)(2,1)}), bf16[32,2,1,12,896]{4,1,3,2,0:T(2,128)(2,1)S(1)}, u32[]{:S(2)}, u32[]{:S(2)}) %all-to-all-start.3) | async-done | bytes 1376288 | tf_op jit(solution)/shard_map/all_to_all | solution.py:40
  299.0 3.4 %copy.55 = f32[32,2,1,12,896]{4,3,1,0,2:T(8,128)} copy(f32[32,2,1,12,896]{4,0,3,2,1:T(8,128)S(1)} %copy_convert_fusion) | data formatting | bytes 5505024 | tf_op jit(solution)/shard_map/convert_element_type | solution.py:89
  302.4 2.9 reshape.110
  305.3 2.7 gather_fusion.1
  307.9 2.9 reshape.120
  310.9 2.7 multiply_reduce_fusion
  313.6 0.7 add_convert_fusion
  (34 shorter events, 2.9 us)
Async XLA Ops:
  6.5 137.7 %copy-start = (bf16[1,256,3584]{2,1,0:T(8,128)(2,1)S(1)}, bf16[1,256,3584]{2,1,0:T(8,128)(2,1)}, u32[]{:S(2)}) copy-start(bf16[1,256,3584]{2,1,0:T(8,128)(2,1)} %param.14) | copy-start | bytes 5505028
  6.5 132.1 %all-gather.3.cloned.1.call-start = ((), (), s32[]{:S(2)}) async-start(), calls=%async_computation.6 | async-start | bytes 6881280 | tf_op jit(solution)/shard_map/all_gather | solution.py:77
  73.2 1.4 copy-start.3
  75.9 85.7 %all-to-all-start.4 = ((bf16[4,128,896]{1,2,0:T(8,128)(2,1)}), bf16[4,128,896]{1,2,0:T(8,128)(2,1)S(1)}, u32[]{:S(2)}, u32[]{:S(2)}) async-start(bf16[4,128,896]{1,2,0:T(8,128)(2,1)} %broadcast_in_dim.25), calls=%async_computation.4 | async-start | bytes 1835008 | tf_op jit(solution)/shard_map/all_to_all | solution.py:18
  161.6 5.5 %copy-start.2 = (bf16[3584,256]{1,0:T(8,128)(2,1)S(1)}, bf16[3584,256]{1,0:T(8,128)(2,1)}, u32[]{:S(2)}) copy-start(bf16[3584,256]{1,0:T(8,128)(2,1)} %param.15) | copy-start | bytes 5505028
  161.6 68.5 %all-to-all-start.1 = ((bf16[4,64,1,12,896]{4,1,3,2,0:T(8,128)(2,1)}), bf16[4,64,1,12,896]{4,1,3,2,0:T(8,128)(2,1)}, u32[]{:S(2)}, u32[]{:S(2)}) async-start(bf16[4,64,1,12,896]{4,1,3,2,0:T(8,128)(2,1)} %bitcast.82), calls=%async_computation.1 | async-start | bytes 11010048 | tf_op jit(solution)/shard_map/all_to_all | solution.py:32
  239.3 17.7 %all-to-all-start.5 = ((bf16[4,128,896]{2,1,0:T(8,128)(2,1)}), bf16[4,128,896]{2,1,0:T(8,128)(2,1)S(1)}, u32[]{:S(2)}, u32[]{:S(2)}) async-start(bf16[4,128,896]{2,1,0:T(8,128)(2,1)} %bitcast.81), calls=%async_computation.5 | async-start | bytes 1835008 | tf_op jit(solution)/shard_map/all_to_all | solution.py:32
  245.3 18.8 %copy-start.4 = (bf16[128,4]{0,1:T(4,128)(2,1)S(1)}, bf16[128,4]{0,1:T(4,128)(2,1)}, u32[]{:S(2)}) copy-start(bf16[128,4]{0,1:T(4,128)(2,1)} %param.11) | copy-start | bytes 3076
  257.1 41.6 %all-to-all-start.3 = ((bf16[32,2,1,12,896]{4,1,3,2,0:T(2,128)(2,1)}), bf16[32,2,1,12,896]{4,1,3,2,0:T(2,128)(2,1)S(1)}, u32[]{:S(2)}, u32[]{:S(2)}) async-start(bf16[32,2,1,12,896]{4,1,3,2,0:T(2,128)(2,1)} %copy.53), calls=%async_computation.3 | async-start | bytes 2752512 | tf_op jit(solution)/shard_map/all_to_all | solution.py:40
  307.9 6.4 %copy-start.1 = (bf16[1,256,3584]{2,1,0:T(8,128)(2,1)S(1)}, bf16[1,256,3584]{2,1,0:T(8,128)(2,1)}, u32[]{:S(2)}) copy-start(bf16[1,256,3584]{2,1,0:T(8,128)(2,1)} %param.14) | copy-start | bytes 5505028
Sparse Core Ops, SparseCore 0:
  74.8 63.8 all-gather.2
where the time goes:
time: 322 us; the launch traced here: 321 us
  waiting for transfers between devices  163 us (51%)
  blocking collectives  60.9 us (19%)
  local copies, waits for them, and re-layouts  33.1 us (10%)
  matrix products  20.8 us (6%)
  starting transfers between devices  20.3 us (6%)
  between operations  13.6 us (4%)
  other arithmetic  9.92 us (3%)
    all_to_all x2, waiting for transfers between devices, sent_and_summed(): lax.all_to_all(tiles, axis, split_axis=0, concat_axis=0, tiled=True)  70.1 us
    all_gather x1, waiting for transfers between devices, per_device(): block_rows = lax.all_gather(arrived, 'tensor', axis=3, tiled=True)  58.3 us
    all_to_all x1, blocking collectives, per_device(): lax.all_to_all(outgoing, EXPERT, split_axis=0, concat_axis=0, tiled=True)  56 us
    all_to_all x1, waiting for transfers between devices, turned_blocks(): lax.all_to_all(tiles, axes[k], split_axis=k, concat_axis=k, tiled=True)  34.2 us
    dot_general x1, matrix products, per_device(): jnp.einsum('sjcf,jfd->sjcd', hidden, w_down, preferred_element_type=jnp.f...  11.5 us
    all_to_all x2, starting transfers between devices, sent_and_summed(): lax.all_to_all(tiles, axis, split_axis=0, concat_axis=0, tiled=True)  8.94 us
    all_to_all x1, starting transfers between devices, turned_blocks(): lax.all_to_all(tiles, axes[k], split_axis=k, concat_axis=k, tiled=True)  6.87 us
    reshape x2, local copies, waits for them, and re-layouts, in_blocks(): return jnp.moveaxis(x.reshape(*before, devices, -1, *after), dim, 0)  6.86 us
  transfers between devices with their start and end apart: 5, of which 4 were waited for; matrix products, arithmetic and copies ran while one was open for 10% of the time, Pallas kernels for 0%

commit v1 on v0

--- a/solution.py
+++ b/solution.py
@@ -74,7 +74,10 @@
     outgoing = padded[owners].reshape(lane_count, per_lane * capacity, narrow)
     arrived = lax.all_to_all(outgoing, EXPERT, split_axis=0, concat_axis=0, tiled=True)
     arrived = arrived.reshape(lane_count, per_lane, capacity, narrow)
-    block_rows = lax.all_gather(arrived, "tensor", axis=3, tiled=True)
+    k_all = lax.axis_size("tensor")
+    blocks_here = [k_all if i0 == 3 else 1 for i0 in range(arrived.ndim)]
+    even = jnp.tile(arrived, blocks_here)
+    block_rows = lax.all_to_all(even, "tensor", split_axis=3, concat_axis=3, tiled=True)
     gate_more = jnp.einsum("sjcd,jdf->sjcf", block_rows, w_gate, preferred_element_type=jnp.float32)
     up_more = jnp.einsum("sjcd,jdf->sjcf", block_rows, w_up, preferred_element_type=jnp.float32)
     hidden = (jax.nn.silu(gate_more) * up_more).astype(jnp.bfloat16)

time: 322 us -> 373 us (1.16)
  local copies, waits for them, and re-layouts: 33.1 us -> 87.3 us
  between operations: 13.6 us -> 0.22 us
  starting transfers between devices: 20.3 us -> 25 us
  waiting for transfers between devices: 163 us -> 167 us
    all_to_all x0 -> x1, waiting for transfers between devices: none -> 63.3 us  [per_device(): lax.all_to_all(even, 'tensor', split_axis=3, concat_axis=3, tiled=True)]
    all_gather x1 -> x0, waiting for transfers between devices: 58.3 us -> none  [per_device(): block_rows = lax.all_gather(arrived, 'tensor', axis=3, tiled=True)]
    unnamed x11 -> x13, local copies, waits for them, and re-layouts: 0.19 us -> 23.6 us
    all_to_all x0 -> x1, local copies, waits for them, and re-layouts: none -> 15.6 us  [per_device(): lax.all_to_all(even, 'tensor', split_axis=3, concat_axis=3, tiled=True)]
    another operation x0 -> x1, local copies, waits for them, and re-layouts: none -> 8.58 us  [per_device(): even = jnp.tile(arrived, blocks_here)]
    all_to_all x1, local copies, waits for them, and re-layouts: 1.42 us -> 8.03 us  [per_device(): lax.all_to_all(outgoing, EXPERT, split_axis=0, concat_axis=0, tiled=True)]
    all_to_all x0 -> x1, starting transfers between devices: none -> 5.25 us  [per_device(): lax.all_to_all(even, 'tensor', split_axis=3, concat_axis=3, tiled=True)]
  transfers between devices with their start and end apart: 5 -> 5, of which waited for: 4 -> 4; matrix products, arithmetic and copies ran while one was open for 10% -> 16% of each run, Pallas kernels for 0% -> 0%
where the time goes in v1:
time: 373 us; the launch traced here: 371 us
  waiting for transfers between devices  167 us (45%)
  local copies, waits for them, and re-layouts  87.3 us (23%)
  blocking collectives  61 us (16%)
  starting transfers between devices  25 us (7%)
  matrix products  20.8 us (6%)
  other arithmetic  9.92 us (3%)
    all_to_all x2, waiting for transfers between devices, sent_and_summed(): lax.all_to_all(tiles, axis, split_axis=0, concat_axis=0, tiled=True)  69.3 us
    all_to_all x1, waiting for transfers between devices, per_device(): lax.all_to_all(even, 'tensor', split_axis=3, concat_axis=3, tiled=True)  63.3 us
    all_to_all x1, blocking collectives, per_device(): lax.all_to_all(outgoing, EXPERT, split_axis=0, concat_axis=0, tiled=True)  56.1 us
    all_to_all x1, waiting for transfers between devices, turned_blocks(): lax.all_to_all(tiles, axes[k], split_axis=k, concat_axis=k, tiled=True)  34.2 us
    unnamed x13, local copies, waits for them, and re-layouts  23.6 us
    all_to_all x1, local copies, waits for them, and re-layouts, per_device(): lax.all_to_all(even, 'tensor', split_axis=3, concat_axis=3, tiled=True)  15.6 us
    dot_general x1, matrix products, per_device(): jnp.einsum('sjcf,jfd->sjcd', hidden, w_down, preferred_element_type=jnp.f...  11.5 us
    all_to_all x2, starting transfers between devices, sent_and_summed(): lax.all_to_all(tiles, axis, split_axis=0, concat_axis=0, tiled=True)  8.95 us
  transfers between devices with their start and end apart: 5, of which 4 were waited for; matrix products, arithmetic and copies ran while one was open for 16% of the time, Pallas kernels for 0%

profile of v1, /device:TPU:32, one launch (start us, length us, event | category | flops | bytes accessed | tf_op | source)
XLA Modules:
  0.0 371.1 jit_solution(17866235579679472113)
XLA Ops:
  3.0 2.4 scatter_custom_fusion
  6.4 2.8 gather_fusion
  9.2 1.4 reshape.103
  10.6 56.1 %all_to_all.35 = bf16[64,12,896]{2,1,0:T(8,128)(2,1)} all-to-all(bf16[64,12,896]{2,1,0:T(8,128)(2,1)} %reshape.103), channel_id=1, replica_groups=mesh['expert_0'=4,'expert_1'=8,'expert_2'=2,'tensor'=4] {'expert_0','exp..., dimensions={0} | all-to-all | bytes 2752512 | tf_op jit(solution)/shard_map/all_to_all | solution.py:75
  66.8 8.0 %copy.52 = bf16[64,12,896]{0,1,2:T(8,128)(2,1)} copy(bf16[64,12,896]{2,1,0:T(8,128)(2,1)} %all_to_all.35) | data formatting | bytes 2752512 | tf_op jit(solution)/shard_map/all_to_all | solution.py:75
  74.8 8.6 %tile.8 = bf16[64,12,4,896]{0,1,3,2:T(8,128)(2,1)} broadcast(bf16[64,12,896]{0,1,2:T(8,128)(2,1)} %copy.52), dimensions={0,1,3} | broadcast | bytes 6881280 | tf_op jit(solution)/shard_map/tile | solution.py:79
  83.4 11.6 %reshape.145 = bf16[4,2,344064]{2,1,0:T(2,128)(2,1)} reshape(bf16[3584,1,12,64]{3,2,1,0:T(8,128)(2,1)} %bitcast.101) | data formatting | bytes 11010048
  95.0 5.2 %all-to-all-start.1 = ((bf16[4,2,344064]{2,1,0:T(2,128)(2,1)}), bf16[4,2,344064]{2,1,0:T(2,128)(2,1)}, u32[]{:S(2)}, u32[]{:S(2)}) async-start(bf16[4,2,344064]{2,1,0:T(2,128)(2,1)} %reshape.145), calls=%async_computation.1 | async-start | bytes 11010048 | tf_op jit(solution)/shard_map/all_to_all | solution.py:80
  100.4 63.3 %all-to-all-done.1 = bf16[4,2,344064]{2,1,0:T(2,128)(2,1)} async-done(((bf16[4,2,344064]{2,1,0:T(2,128)(2,1)}), bf16[4,2,344064]{2,1,0:T(2,128)(2,1)}, u32[]{:S(2)}, u32[]{:S(2)}) %all-to-all-start.1) | async-done | bytes 5505056 | tf_op jit(solution)/shard_map/all_to_all | solution.py:80
  163.7 1.0 broadcast_in_dim.25
  164.7 3.7 all-to-all-start.5
  168.4 11.8 %reshape.146 = bf16[3584,1,12,64]{3,2,1,0:T(8,128)(2,1)} reshape(bf16[4,2,344064]{2,1,0:T(2,128)(2,1)} %all-to-all-done.1) | data formatting | bytes 11010048
  180.2 15.6 %copy.53 = bf16[64,1,12,3584]{3,0,2,1:T(8,128)(2,1)} copy(bf16[64,1,12,3584]{0,2,1,3:T(8,128)(2,1)} %bitcast.100) | data formatting | bytes 11010048 | tf_op jit(solution)/shard_map/all_to_all | solution.py:80
  195.8 5.6 %fusion.7 = f32[64,1,12,256]{3,0,2,1:T(8,128)} fusion(bf16[1,3584,256]{2,1,0:T(8,128)(2,1)} %param.12, bf16[64,1,12,3584]{3,0,2,1:T(8,128)(2,1)} %copy.53), kind=kOutput, calls=%fused_computation.16 | convolution fusion | flops 1409286144 | bytes 8126464 | tf_op jit(solution)/shard_map/sjcd,jdf->sjcf/dot_general | solution.py:81
  201.5 11.5 %convolution_convert_fusion = bf16[64,12,3584]{2,0,1:T(8,128)(2,1)} fusion(bf16[1,256,3584]{2,1,0:T(8,128)(2,1)S(1)} %copy-done, bf16[1,3584,256]{2,1,0:T(8,128)(2,1)} %param.13, bf16[64,1,12,3584]{3,0,2,1:T(8,128)(2,1)} %copy.53, f32[64,1,12,256]{3,0,2,1:T(8,128)} %fusion.7), kind=kOutput, calls=%fused_computation.3 | convolution fusion | flops 2822504448 | bytes 15466496 | tf_op jit(solution)/shard_map/sjcf,jfd->sjcd/dot_general | solution.py:84
  212.9 5.9 %copy.69 = bf16[1,12,8,4,8,896]{5,4,2,1,0,3:T(8,128)(2,1)} copy(bf16[1,12,8,4,8,896]{5,4,3,2,1,0:T(8,128)(2,1)} %bitcast.105) | data formatting | bytes 11010048 | tf_op jit(solution)/shard_map/reshape | solution.py:27
  218.8 5.2 %all-to-all-start.2 = ((bf16[4,64,1,12,896]{4,1,3,2,0:T(8,128)(2,1)}), bf16[4,64,1,12,896]{4,1,3,2,0:T(8,128)(2,1)}, u32[]{:S(2)}, u32[]{:S(2)}) async-start(bf16[4,64,1,12,896]{4,1,3,2,0:T(8,128)(2,1)} %bitcast.102), calls=%async_computation.2 | async-start | bytes 11010048 | tf_op jit(solution)/shard_map/all_to_all | solution.py:32
  224.5 3.3 convolution_convert_fusion.1
  227.8 1.0 copy.70
  228.8 57.8 %all-to-all-done.2 = bf16[4,64,1,12,896]{4,1,3,2,0:T(8,128)(2,1)} async-done(((bf16[4,64,1,12,896]{4,1,3,2,0:T(8,128)(2,1)}), bf16[4,64,1,12,896]{4,1,3,2,0:T(8,128)(2,1)}, u32[]{:S(2)}, u32[]{:S(2)}) %all-to-all-start.2) | async-done | bytes 5505056 | tf_op jit(solution)/shard_map/all_to_all | solution.py:32
  286.7 3.6 reduce_sum.50
  291.0 4.8 %all_to_all.36 = bf16[32,2,1,12,896]{4,0,3,2,1:T(8,128)(2,1)S(1)} all-to-all(bf16[32,2,1,12,896]{4,0,3,2,1:T(8,128)(2,1)S(1)} %copy.56), channel_id=1, replica_groups=mesh['expert_0'=4,'expert_1'=8,'expert_2'=2,'tensor'=4] {'expert_2'}, dimensions={1} | all-to-all | bytes 2752512 | tf_op jit(solution)/shard_map/all_to_all | solution.py:40
  295.8 3.7 %all-to-all-start.6 = ((bf16[4,128,896]{2,1,0:T(8,128)(2,1)}), bf16[4,128,896]{2,1,0:T(8,128)(2,1)S(1)}, u32[]{:S(2)}, u32[]{:S(2)}) async-start(bf16[4,128,896]{2,1,0:T(8,128)(2,1)} %bitcast.99), calls=%async_computation.6 | async-start | bytes 1835008 | tf_op jit(solution)/shard_map/all_to_all | solution.py:32
  299.6 2.5 copy.57
  302.1 11.5 %all-to-all-done.6 = bf16[4,128,896]{2,1,0:T(8,128)(2,1)S(1)} async-done(((bf16[4,128,896]{2,1,0:T(8,128)(2,1)}), bf16[4,128,896]{2,1,0:T(8,128)(2,1)S(1)}, u32[]{:S(2)}, u32[]{:S(2)}) %all-to-all-start.6) | async-done | bytes 917536 | tf_op jit(solution)/shard_map/all_to_all | solution.py:32
  313.6 7.2 %all-to-all-start.4 = ((bf16[32,2,1,12,896]{4,1,3,2,0:T(2,128)(2,1)}), bf16[32,2,1,12,896]{4,1,3,2,0:T(2,128)(2,1)S(1)}, u32[]{:S(2)}, u32[]{:S(2)}) async-start(bf16[32,2,1,12,896]{4,1,3,2,0:T(2,128)(2,1)} %copy.57), calls=%async_computation.4 | async-start | bytes 2752512 | tf_op jit(solution)/shard_map/all_to_all | solution.py:40
  321.2 34.2 %all-to-all-done.4 = bf16[32,2,1,12,896]{4,1,3,2,0:T(2,128)(2,1)S(1)} async-done(((bf16[32,2,1,12,896]{4,1,3,2,0:T(2,128)(2,1)}), bf16[32,2,1,12,896]{4,1,3,2,0:T(2,128)(2,1)S(1)}, u32[]{:S(2)}, u32[]{:S(2)}) %all-to-all-start.4) | async-done | bytes 1376288 | tf_op jit(solution)/shard_map/all_to_all | solution.py:40
  355.8 3.4 copy.59
  359.2 2.9 reshape.112
  362.1 2.7 gather_fusion.1
  364.8 2.9 reshape.122
  367.7 2.7 multiply_reduce_fusion
  (37 shorter events, 6.8 us)
Async XLA Ops:
  0.0 201.5 %copy-start = (bf16[1,256,3584]{2,1,0:T(8,128)(2,1)S(1)}, bf16[1,256,3584]{2,1,0:T(8,128)(2,1)}, u32[]{:S(2)}) copy-start(bf16[1,256,3584]{2,1,0:T(8,128)(2,1)} %param.14) | copy-start | bytes 5505028
  95.0 5.3 %copy-start.3 = (bf16[128,896]{1,0:T(8,128)(2,1)S(1)}, bf16[128,896]{1,0:T(8,128)(2,1)}, u32[]{:S(2)}) copy-start(bf16[128,896]{1,0:T(8,128)(2,1)} %param.9) | copy-start | bytes 688132
  95.0 68.7 %all-to-all-start.1 = ((bf16[4,2,344064]{2,1,0:T(2,128)(2,1)}), bf16[4,2,344064]{2,1,0:T(2,128)(2,1)}, u32[]{:S(2)}, u32[]{:S(2)}) async-start(bf16[4,2,344064]{2,1,0:T(2,128)(2,1)} %reshape.145), calls=%async_computation.1 | async-start | bytes 11010048 | tf_op jit(solution)/shard_map/all_to_all | solution.py:80
  164.7 54.1 %all-to-all-start.5 = ((bf16[4,128,896]{1,2,0:T(8,128)(2,1)}), bf16[4,128,896]{1,2,0:T(8,128)(2,1)S(1)}, u32[]{:S(2)}, u32[]{:S(2)}) async-start(bf16[4,128,896]{1,2,0:T(8,128)(2,1)} %broadcast_in_dim.25), calls=%async_computation.5 | async-start | bytes 1835008 | tf_op jit(solution)/shard_map/all_to_all | solution.py:18
  218.8 5.2 %copy-start.2 = (bf16[3584,256]{1,0:T(8,128)(2,1)S(1)}, bf16[3584,256]{1,0:T(8,128)(2,1)}, u32[]{:S(2)}) copy-start(bf16[3584,256]{1,0:T(8,128)(2,1)} %param.15) | copy-start | bytes 5505028
  218.8 67.8 %all-to-all-start.2 = ((bf16[4,64,1,12,896]{4,1,3,2,0:T(8,128)(2,1)}), bf16[4,64,1,12,896]{4,1,3,2,0:T(8,128)(2,1)}, u32[]{:S(2)}, u32[]{:S(2)}) async-start(bf16[4,64,1,12,896]{4,1,3,2,0:T(8,128)(2,1)} %bitcast.102), calls=%async_computation.2 | async-start | bytes 11010048 | tf_op jit(solution)/shard_map/all_to_all | solution.py:32
  295.8 17.7 %all-to-all-start.6 = ((bf16[4,128,896]{2,1,0:T(8,128)(2,1)}), bf16[4,128,896]{2,1,0:T(8,128)(2,1)S(1)}, u32[]{:S(2)}, u32[]{:S(2)}) async-start(bf16[4,128,896]{2,1,0:T(8,128)(2,1)} %bitcast.99), calls=%async_computation.6 | async-start | bytes 1835008 | tf_op jit(solution)/shard_map/all_to_all | solution.py:32
  302.1 18.9 %copy-start.4 = (bf16[128,4]{0,1:T(4,128)(2,1)S(1)}, bf16[128,4]{0,1:T(4,128)(2,1)}, u32[]{:S(2)}) copy-start(bf16[128,4]{0,1:T(4,128)(2,1)} %param.11) | copy-start | bytes 3076
  313.6 41.9 %all-to-all-start.4 = ((bf16[32,2,1,12,896]{4,1,3,2,0:T(2,128)(2,1)}), bf16[32,2,1,12,896]{4,1,3,2,0:T(2,128)(2,1)S(1)}, u32[]{:S(2)}, u32[]{:S(2)}) async-start(bf16[32,2,1,12,896]{4,1,3,2,0:T(2,128)(2,1)} %copy.57), calls=%async_computation.4 | async-start | bytes 2752512 | tf_op jit(solution)/shard_map/all_to_all | solution.py:40
  364.8 6.4 %copy-start.1 = (bf16[1,256,3584]{2,1,0:T(8,128)(2,1)S(1)}, bf16[1,256,3584]{2,1,0:T(8,128)(2,1)}, u32[]{:S(2)}) copy-start(bf16[1,256,3584]{2,1,0:T(8,128)(2,1)} %param.14) | copy-start | bytes 5505028
